TPU v7x, 256 devices: a whole 4x4x8 slice. The times are simulated.
256 devices in a mesh: vocab: 32 (over z_hi, x, y), batch: 8 (over z_lo, core).
Axes of the slice: x: 4, y: 4, z: 8 (z_hi: 2, z_lo: 4; z = z_hi * 4 + z_lo), core: 2. Of those that a mesh axis runs over, the one named last changes fastest.
Arguments:
- draft_hidden: bfloat16 [128, 4096], P('vocab', 'batch')
- target_hidden: bfloat16 [128, 8192], P('vocab', 'batch')
- draft_gain: float32 [4096], P('batch'), may hold values from 0.5 to 1.5
- target_gain: float32 [8192], P('batch'), may hold values from 0.5 to 1.5
- draft_head: bfloat16 [4096, 128256], P('batch', 'vocab')
- target_head: bfloat16 [8192, 128256], P('batch', 'vocab')
- token_class: int32 [128256], P('vocab'), may hold values from 0 to 29
- grammar_bits: int32 [128], replicated, may hold values from 0 to 1073741823
- draft_tokens: int32 [128], replicated, may hold values from 0 to 128255
Outputs:
- log_ratio: float32 [128], P('batch')
- target_logprob: float32 [128], P('batch')
Inputs may be any that keep to these rules, and one draw needn't show every extreme that they name: `token_class`: a class number of 0 to 29 for each vocabulary entry. `grammar_bits`: bits 0 to 29 in use.
All inputs are finite; a program needn't handle non-finite values.
Results may differ from a plain program's by a relative error of at most 0.00042.
Values may be sent and summed in bfloat16 or wider, within the bound.
A program may use at most 64 MiB of HBM per device.

v0:
```python
import jax
import jax.numpy as jnp
from jax import lax
from jax.sharding import PartitionSpec as P

D_DRAFT = 4096
D_TARGET = 8192


eps_norm = 1e-05
neg_fill = -1e30


def sent_to_all(value, axis):
    length = lax.axis_size(axis)
    return lax.all_to_all(
        jnp.broadcast_to(value[None], (length, *value.shape)), axis, 0, 0, tiled=True
    )


def over_copies(value, axis):
    everything = sent_to_all(value, axis)
    return jnp.sum(everything, axis=0)


def packed_total(arrays, axis):
    flat, at, gathered = (jnp.concatenate([a.reshape(-1) for a in arrays]), 0, [])
    running = over_copies(flat, axis)
    for a in arrays:
        gathered.append(running[at : at + a.size].reshape(a.shape))
        at += a.size
    return tuple(gathered)


def joined_along(blocks, dim):
    dims = list(blocks.shape[1:])
    dims[dim] *= blocks.shape[0]
    return jnp.moveaxis(blocks, 0, dim).reshape(dims)


def gather_directly(value, axis, dim):
    return joined_along(sent_to_all(value, axis), dim)


def sent_together(arrays, axis, dim, along):
    both = jnp.concatenate(arrays, axis=along)
    whole, at, gathered = (gather_directly(both, axis, dim), 0, [])
    for a in arrays:
        gathered.append(lax.slice_in_dim(whole, at, at + a.shape[along], axis=along))
        at += a.shape[along]
    return tuple(gathered)


def sent_together_2(arrays, axis, dim, along):
    widths = [a.shape[along] for a in arrays]
    both = jnp.concatenate(arrays, axis=along)
    whole = lax.psum_scatter(both, axis, scatter_dimension=dim, tiled=True)
    return tuple(jnp.split(whole, [sum(widths[:k]) for k in range(1, len(widths))], axis=along))


def all_in_one(value, axis):
    leaves = jax.tree.leaves(value)
    sequence = sorted(range(len(leaves)), key=lambda k: -leaves[k].size)
    width = (1, *leaves[sequence[0]].shape)[-1]
    lines = [
        jnp.pad(leaves[k].reshape(-1), (0, -leaves[k].size % width)).reshape(-1, width)
        for k in sequence
    ]
    both, at, found = (sent_to_all(jnp.concatenate(lines), axis), 0, {})
    for k, line in zip(sequence, lines):
        piece = both[:, at : at + len(line)].reshape(len(both), -1)
        found[k] = piece[:, : leaves[k].size].reshape(-1, *leaves[k].shape)
        at += len(line)
    numbers = iter(range(len(leaves)))
    return jax.tree.map(lambda _: found[next(numbers)], value)


def folded_in_pairs(pieces, combine):
    while len(jax.tree.leaves(pieces)[0]) > 1:
        pieces = jax.vmap(combine)(
            *(jax.tree.map(lambda part: part[side::2], pieces) for side in (0, 1))
        )
    return jax.tree.map(lambda part: part[0], pieces)


def merged_2(value, axis, combine):
    pieces = all_in_one(value, axis)
    return folded_in_pairs(pieces, combine)


def scale_rows(values, squares, width, gain_vec):
    scale = lax.rsqrt(squares[:, None] / width + eps_norm)
    return (values * scale * gain_vec[None, :]).astype(jnp.bfloat16)


def shard_stats(logits, allowed, chosen):
    masked = jnp.where(allowed, logits, neg_fill)
    highest = jnp.max(masked, axis=1)
    summed = jnp.sum(jnp.where(allowed, jnp.exp(masked - highest[:, None]), 0.0), axis=1)
    picked = jnp.sum(jnp.where(chosen, logits, 0.0), axis=1)
    return (highest, summed, picked)


def join_pair(highest_a, summed_a, highest_b, summed_b):
    highest = jnp.maximum(highest_a, highest_b)
    summed = summed_a * jnp.exp(highest_a - highest) + summed_b * jnp.exp(highest_b - highest)
    return (highest, summed)


def join_every(first, other):
    draft_part = join_pair(first[0], first[1], other[0], other[1])
    target_part = join_pair(first[2], first[3], other[2], other[3])
    return (
        draft_part[0],
        draft_part[1],
        target_part[0],
        target_part[1],
        first[4] + other[4],
        first[5] + other[5],
    )


def local_stats(draft_logits, target_logits, bits_here, tokens_here, classes, column_start):
    width = classes.shape[0]
    columns = column_start + lax.broadcasted_iota(jnp.int32, (1, width), 1)
    chosen = columns == tokens_here[:, None]
    allowed = (bits_here[:, None] >> classes[None, :] & 1 == 1) | chosen
    draft_high, draft_sum, draft_pick = shard_stats(draft_logits, allowed, chosen)
    target_high, target_sum, target_pick = shard_stats(target_logits, allowed, chosen)
    return (draft_high, draft_sum, target_high, target_sum, draft_pick, target_pick)


def finish(merged):
    draft_high, draft_sum, target_high, target_sum, draft_pick, target_pick = merged
    target_logprob = target_pick - (target_high + jnp.log(target_sum))
    log_ratio = target_logprob - (draft_pick - (draft_high + jnp.log(draft_sum)))
    return (log_ratio, target_logprob)


def shards(
    draft_hidden,
    target_hidden,
    draft_gain,
    target_gain,
    draft_head,
    target_head,
    token_class,
    grammar_bits,
    draft_tokens,
):
    batch_count = lax.axis_size("batch")
    shard_width = draft_head.shape[1]
    draft_values = draft_hidden.astype(jnp.float32)
    target_values = target_hidden.astype(jnp.float32)
    draft_square, target_square = packed_total(
        (
            jnp.sum(draft_values * draft_values, axis=1),
            jnp.sum(target_values * target_values, axis=1),
        ),
        "batch",
    )
    draft_normed = scale_rows(draft_values, draft_square, D_DRAFT, draft_gain)
    target_normed = scale_rows(target_values, target_square, D_TARGET, target_gain)
    pieces = sent_together((draft_normed, target_normed), "vocab", 0, 1)
    draft_pieces = pieces[0]
    target_pieces = pieces[1]
    joined = jnp.concatenate(
        [
            jnp.dot(draft_pieces, draft_head, preferred_element_type=jnp.float32),
            jnp.dot(target_pieces, target_head, preferred_element_type=jnp.float32),
        ],
        axis=1,
    )
    draft_partial = joined[:, :shard_width]
    target_partial = joined[:, shard_width:]
    total_rows = grammar_bits.shape[0]
    block_rows = total_rows // batch_count
    row_start = lax.axis_index("batch") * block_rows
    draft_logits, target_logits = sent_together_2((draft_partial, target_partial), "batch", 0, 1)
    bits_here = lax.dynamic_slice_in_dim(grammar_bits, row_start, block_rows, 0)
    tokens_here = lax.dynamic_slice_in_dim(draft_tokens, row_start, block_rows, 0)
    column_start = lax.axis_index("vocab") * shard_width
    stats = local_stats(
        draft_logits, target_logits, bits_here, tokens_here, token_class, column_start
    )
    merged = merged_2(stats, "vocab", join_every)
    return finish(merged)


def solution(mesh):
    in_specs = (
        P("vocab", "batch"),
        P("vocab", "batch"),
        P("batch"),
        P("batch"),
        P("batch", "vocab"),
        P("batch", "vocab"),
        P("vocab"),
        P(),
        P(),
    )
    out_specs = (P("batch"), P("batch"))
    return jax.shard_map(shards, mesh=mesh, in_specs=in_specs, out_specs=out_specs, check_vma=False)
```

profile of v0, /device:TPU:8, one launch (start us, length us, event | category | flops | bytes accessed | tf_op | source)
XLA Modules:
  0.0 154.0 jit_solution(18381161790885466607)
XLA Ops:
  7.2 0.0 reduce-scatter.4.cloned.1.call-start
  7.2 0.8 fusion.8
  8.0 0.8 fusion.11
  8.8 0.1 pad_maximum_fusion.2
  8.9 11.3 %all_to_all.16 = f32[8,1,8]{2,1,0:T(1,128)S(1)} all-to-all(f32[8,1,8]{2,1,0:T(1,128)S(1)} %broadcast_in_dim.17), channel_id=1, replica_groups=mesh['vocab'=32,'batch'=8] {'batch'}, dimensions={0} | all-to-all | bytes 512 | tf_op jit(solution)/shard_map/all_to_all | solution.py:16
  20.2 0.1 add_rsqrt_fusion.1
  20.3 0.8 fusion.10
  21.1 0.8 fusion.13
  21.9 0.1 broadcast_in_dim.18
  22.0 26.2 %all_to_all.17 = bf16[32,4,1536]{2,1,0:T(4,128)(2,1)S(1)} all-to-all(bf16[32,4,1536]{2,1,0:T(4,128)(2,1)S(1)} %broadcast_in_dim.18), channel_id=1, replica_groups=mesh['vocab'=32,'batch'=8] {'vocab'}, dimensions={0} | all-to-all | bytes 786432 | tf_op jit(solution)/shard_map/all_to_all | solution.py:16
  48.1 0.1 reshape.77
  48.2 0.0 copy-start.1
  48.2 4.9 %fusion.4 = f32[128,4008]{0,1:T(8,128)S(1)} fusion(bf16[1024,4008]{0,1:T(8,128)(2,1)} %param.14, bf16[128,1536]{1,0:T(8,128)(2,1)S(1)} %reshape.77), kind=kOutput, calls=%fused_computation.13 | convolution fusion | flops 1050673152 | bytes 10522624 | tf_op jit(solution)/shard_map/dot_general | solution.py:170
  53.2 0.0 copy-done.1
  53.2 1.2 fusion.6
  54.4 2.2 %pad_maximum_fusion = f32[128,8016]{0,1:T(8,128)} fusion(f32[128,4008]{0,1:T(8,128)S(1)} %fusion.4, f32[128,4008]{0,1:T(8,128)S(1)} %fusion.6), kind=kLoop, calls=%fused_computation | loop fusion | flops 1026048 | bytes 8208384 | tf_op jit(solution)/shard_map/concatenate | solution.py:56
  56.6 5.6 %copy.24 = f32[128,8016]{1,0:T(8,128)} copy(f32[128,8016]{0,1:T(8,128)} %pad_maximum_fusion) | data formatting | bytes 8208384
  62.2 0.0 copy-start.3
  62.2 0.0 copy-start.4
  62.2 0.0 reduce-scatter.4.cloned.1.call-update
  62.3 0.6 copy-done.3
  62.9 0.1 dynamic_slice.7
  62.9 0.0 copy-done.4
  63.0 0.1 dynamic_slice.6
  63.0 49.9 %reduce-scatter.4.cloned.1.call-done = f32[16,8016]{1,0:T(8,128)} async-done(((f32[128,8016]{1,0:T(8,128)}), f32[16,8016]{1,0:T(8,128)}) %reduce-scatter.4.cloned.1.call-update) | async-done | bytes 513040
  113.0 1.2 fusion.18
  114.1 0.0 copy-start.2
  114.1 0.6 copy.27
  114.7 1.9 %copy.26 = f32[16,4008]{0,1:T(8,128)} copy(f32[16,4008]{1,0:T(8,128)S(1)} %get-tuple-element.28) | data formatting | bytes 513024
  116.7 0.0 copy-done.2
  116.7 0.0 copy-start
  116.7 4.7 %fusion.3 = (f32[16]{0:T(128)S(1)}, f32[16]{0:T(128)S(1)}) fusion(f32[16,4008]{0,1:T(8,128)S(1)} %copy.27, s32[16]{0:T(128)S(1)} %dynamic_slice.7, s32[4008]{0:T(1024)S(1)} %iota_add_fusion, s32[4008]{0:T(1024)S(1)} %copy-done.2, s32[16]{0:T(128)S(1)} %dynamic_slice.6, f32[16,4008]{0,1:T(8,128)} %copy.26), kind=kLoop, calls=%fused_computation.12 | loop fusion | flops 577120 | bytes 545344 | tf_op jit(solution)/shard_map/reduce_max | solution.py:98
  121.4 0.0 copy-done
  121.4 2.8 %fusion = (f32[16]{0:T(128)S(1)}, f32[16]{0:T(128)S(1)}, f32[16]{0:T(128)S(1)}, f32[16]{0:T(128)S(1)}) fusion(f32[16,4008]{0,1:T(8,128)S(1)} %copy-done, s32[16]{0:T(128)S(1)} %dynamic_slice.7, s32[4008]{0:T(1024)S(1)} %iota_add_fusion, f32[16]{0:T(128)S(1)} %get-tuple-element.9, s32[4008]{0:T(1024)S(1)} %copy-done.2, s32[16]{0:T(128)S(1)} %dynamic_slice.6, ...), kind=kLoop, calls=%fused_computation.4 | loop fusion | flops 1090112 | bytes 545600 | tf_op jit(solution)/shard_map/reduce_sum | solution.py:100
  124.3 21.1 %all_to_all.18 = f32[32,6,16]{2,1,0:T(8,128)S(1)} all-to-all(f32[32,6,16]{2,1,0:T(8,128)S(1)} %broadcast_in_dim.21), channel_id=1, replica_groups=mesh['vocab'=32,'batch'=8] {'vocab'}, dimensions={0} | all-to-all | bytes 24576 | tf_op jit(solution)/shard_map/all_to_all | solution.py:16
  145.4 0.1 fusion.19
  146.6 0.5 bitcast_subtract_fusion
  (69 shorter events, 1.1 us)
Async XLA Ops:
  7.2 105.8 %reduce-scatter.4.cloned.1.call-start = ((), (), s32[]{:S(2)}) async-start(), calls=%async_computation.4 | async-start | bytes 4644864
  48.2 4.9 %copy-start.1 = (bf16[512,4008]{0,1:T(8,128)(2,1)S(1)}, bf16[512,4008]{0,1:T(8,128)(2,1)}, u32[]{:S(2)}) copy-start(bf16[512,4008]{0,1:T(8,128)(2,1)} %param.13) | copy-start | bytes 12312580
  62.2 0.7 copy-start.3
  62.2 0.7 copy-start.4
  114.1 2.6 %copy-start.2 = (s32[4008]{0:T(1024)S(1)}, s32[4008]{0:T(1024)}, u32[]{:S(2)}) copy-start(s32[4008]{0:T(1024)} %param.15) | copy-start | bytes 48100
  116.7 4.7 %copy-start = (f32[16,4008]{0,1:T(8,128)S(1)}, f32[16,4008]{0,1:T(8,128)}, u32[]{:S(2)}) copy-start(f32[16,4008]{0,1:T(8,128)} %copy.26) | copy-start | bytes 769540
Sparse Core Ops, SparseCore 0:
  62.4 50.5 reduce-scatter.3
where the time goes:
time: 155 us; the launch traced here: 154 us
  blocking collectives  58.6 us (38%)
  waiting for transfers between devices  49.9 us (32%)
  between operations  14.2 us (9%)
  other arithmetic  13.8 us (9%)
  local copies, waits for them, and re-layouts  11.3 us (7%)
  matrix products  6.15 us (4%)
    all_to_all x3, blocking collectives, sent_to_all(): lax.all_to_all(jnp.broadcast_to(value[None], (length, *value.shape)), axi...  58.6 us
    unnamed x2, waiting for transfers between devices  49.9 us
    unnamed x13, local copies, waits for them, and re-layouts  8.79 us
    dot_general x1, matrix products, shards(): jnp.dot(target_pieces, target_head, preferred_element_type=jnp.float32)  4.9 us
    reduce_max x1, other arithmetic, shard_stats(): highest = jnp.max(masked, axis=1)  4.74 us
  transfers between devices with their start and end apart: 1, of which 1 were waited for; matrix products, arithmetic and copies ran while one was open for 0% of the time, Pallas kernels for 0%

commit v1 on v0

v1 whole, which is shorter than its diff:
```python
import functools
import math

import jax
import jax.numpy as jnp
from jax import lax
from jax.experimental import pallas as pl
from jax.experimental.pallas import tpu as pltpu
from jax.sharding import PartitionSpec as P

D_DRAFT = 4096
D_TARGET = 8192
EPS = 1e-05
NEG = -1e30
F32 = jnp.float32
BF16 = jnp.bfloat16

PLANE = 16
CHAIN = 4
ROWS = 128
HALF = 64
BLOCK = 16
CW = 1024
Q = 4
PER_STAGE = 2 * Q
CHUNKS = 2 * PER_STAGE
LAG = 1
HOP = 3
WSPLIT = 1024
LEVELS = 32760.0


def kernel(
    dims,
    dh, th, dg, tg, wd_hbm, wt_hbm, cls_hbm, bits_hbm, tok_hbm,
    ratio_ref, logprob_ref,
    xg, gain, wd, wt, cls_in, cls, colid, bits_s, tok_s,
    xf, xn, srow, ssib, pb, pr, sb, rb, qs, qr, hs, hr, fb, bt, st,
    grow, gall, zrow, zall,
    load_sem, w_sem, near_send, far_send, pair_send, g_recv,
    d2_send, d2_recv, sib_send, sib_recv,
    c_send, c_recv, q_send, q_recv, h_send, h_recv,
    fin_send, fin_recv, z_send, z_recv,
):
    kd, kt, width = dims
    kk = kd + kt
    v = lax.axis_index("vocab")
    b = lax.axis_index("batch")
    half = v // PLANE
    place = v % PLANE
    chip = b // 2
    core = b % 2
    mate = chip * 2 + (1 - core)
    partner = (v + PLANE) % (2 * PLANE)

    def remote(src, dst, send, recv, vv, bb):
        return pltpu.make_async_remote_copy(
            src_ref=src, dst_ref=dst, send_sem=send, recv_sem=recv,
            device_id=(vv, bb), device_id_type=pl.DeviceIdType.MESH,
        )

    loads = [
        pltpu.make_async_copy(dh, xg.at[v, :, 0:kd], load_sem.at[0]),
        pltpu.make_async_copy(th, xg.at[v, :, kd:kk], load_sem.at[1]),
        pltpu.make_async_copy(dg, gain.at[:, 0:kd], load_sem.at[2]),
        pltpu.make_async_copy(tg, gain.at[:, kd:kk], load_sem.at[3]),
        pltpu.make_async_copy(cls_hbm, cls_in, load_sem.at[4]),
        pltpu.make_async_copy(bits_hbm, bits_s, load_sem.at[5]),
        pltpu.make_async_copy(tok_hbm, tok_s, load_sem.at[6]),
    ]
    for copy in loads:
        copy.start()

    barrier = pltpu.get_barrier_semaphore()

    def greet(vv, bb):
        pl.semaphore_signal(
            barrier, inc=1, device_id=(vv, bb), device_id_type=pl.DeviceIdType.MESH
        )

    def greet_plane(t, carry):
        greet(half * PLANE + (place + t) % PLANE, b)
        return carry

    def greet_line(t, carry):
        zz = (half * CHAIN + chip + t) % (2 * CHAIN)
        greet((zz // CHAIN) * PLANE + place, (zz % CHAIN) * 2 + core)
        return carry

    lax.fori_loop(1, 2 * CHAIN, greet_line, 0)
    lax.fori_loop(1, PLANE, greet_plane, 0)
    greet(v, mate)

    weights = []
    for hbm, ref in ((wd_hbm, wd), (wt_hbm, wt)):
        for at in range(0, width, WSPLIT):
            rows = pl.ds(at, min(WSPLIT, width - at))
            weights.append((hbm.at[rows], ref.at[rows]))
    weights = [
        pltpu.make_async_copy(src, dst, w_sem.at[n]) for n, (src, dst) in enumerate(weights)
    ]
    for copy in weights:
        copy.start()

    pl.semaphore_wait(barrier, (2 * CHAIN - 1) + (PLANE - 1) + 1)

    loads[0].wait()
    loads[1].wait()
    to_partner = remote(xg.at[v], xg.at[v], pair_send.at[0], g_recv.at[v], partner, b)
    to_partner.start()

    def near_copy(t):
        return remote(
            xg.at[v], xg.at[v], near_send.at[t], g_recv.at[v],
            half * PLANE + (place + t) % PLANE, b,
        )

    def far_copy(t):
        return remote(
            xg.at[partner], xg.at[partner], far_send.at[t], g_recv.at[partner],
            half * PLANE + (place + t) % PLANE, b,
        )

    def arrived(vv):
        remote(xg.at[vv], xg.at[vv], pair_send.at[0], g_recv.at[vv], v, b).wait_recv()

    def start_near(t, carry):
        near_copy(t).start()
        return carry

    def start_far(t, carry):
        far_copy(t).start()
        return carry

    lax.fori_loop(1, PLANE, start_near, 0)

    for copy in loads[2:]:
        copy.wait()
    lanes_all = lax.broadcasted_iota(jnp.int32, (1, Q * CW), 1)
    colid[...] = jnp.where(lanes_all < width, lanes_all, -(1 << 30))
    cls[...] = jnp.full((1, Q * CW), 30, jnp.int32)
    cls[:, 0:width] = cls_in[...]
    lane = lax.broadcasted_iota(jnp.int32, (BLOCK, 128), 1)
    sub = lax.broadcasted_iota(jnp.int32, (BLOCK, 128), 0)
    for a in range(2):
        stage = half if a == 0 else 1 - half
        at = (stage * 4 + (chip // 2) * 2 + core) * BLOCK
        bits_col = jnp.zeros((BLOCK, 128), jnp.int32)
        tok_col = jnp.zeros((BLOCK, 128), jnp.int32)
        for r in range(BLOCK):
            bits_col = jnp.where(sub == r, bits_s[at + r], bits_col)
            tok_col = jnp.where(sub == r, tok_s[at + r], tok_col)
        bt[a, 0] = bits_col
        bt[a, 1] = tok_col - v * width
        for m in range(2):
            st[a * 2 + m, 0] = jnp.full((BLOCK, 128), NEG, F32)
            st[a * 2 + m, 1] = jnp.zeros((BLOCK, 128), F32)
            st[a * 2 + m, 2] = jnp.zeros((BLOCK, 128), F32)
    for d in range(2):
        pos = chip if d else (CHAIN - 1) - chip

        @pl.when(pos == 0)
        def _():
            hr[d] = jnp.zeros((2, 1, 128), F32)

    for copy in weights:
        copy.wait()
    wd[width:, :] = jnp.zeros((Q * CW - width, kd), BF16)
    wt[width:, :] = jnp.zeros((Q * CW - width, kt), BF16)

    arrived(partner)
    lax.fori_loop(1, PLANE, start_far, 0)

    def prepare(a):
        stage = half if a == 0 else 1 - half

        def wait_row(t, carry):
            arrived(stage * PLANE + (place + t) % PLANE)
            return carry

        lax.fori_loop(1, PLANE, wait_row, 0)
        for i in range(PLANE):
            xf[4 * i : 4 * i + 4, :] = xg[stage * PLANE + i].astype(F32)
        gv = gain[...]
        total = jnp.zeros((BLOCK, 128), F32)
        for g in range(HALF // BLOCK):
            values = xf[g * BLOCK : (g + 1) * BLOCK, :]
            for m, (lo, hi) in enumerate(((0, kd), (kd, kk))):
                part = values[:, lo:hi]
                square = jnp.sum(part * part, axis=1, keepdims=True) + (hi - lo) * EPS
                scaled = part * lax.rsqrt(square) * gv[:, lo:hi]
                xn[a, g * BLOCK : (g + 1) * BLOCK, lo:hi] = scaled.astype(BF16)
                total = total + jnp.where(lane == sub + (m * HALF + g * BLOCK), square, 0.0)
        srow[a] = jnp.sum(total, axis=0, keepdims=True)
        remote(srow.at[a], ssib.at[a], sib_send.at[a], sib_recv.at[a], v, mate).start()

    def multiply(s):
        a = s // PER_STAGE
        r = s % PER_STAGE
        quarter = r // 2

        def run(ref, lo, hi):
            left = xn[a, :, lo:hi]
            for n in range(CW // 256):
                at = pl.multiple_of(quarter * CW + n * 256, 256)
                out = lax.dot_general(
                    left, ref[pl.ds(at, 256), :], (((1,), (1,)), ((), ())),
                    preferred_element_type=F32,
                )
                for blk in range(HALF // BLOCK):
                    pb[s, blk % 2, blk // 2, :, n * 256 : (n + 1) * 256] = out[
                        blk * BLOCK : (blk + 1) * BLOCK
                    ]

        @pl.when(r % 2 == 0)
        def _():
            run(wd, 0, kd)

        @pl.when(r % 2 == 1)
        def _():
            run(wt, kd, kk)

    def d2_copy(j):
        return remote(pb.at[j, 1 - core], pr.at[j], d2_send.at[j], d2_recv.at[j], v, mate)

    def chain_to(d):
        return (chip + (1 if d else -1)) * 2 + core

    def chunk_copy(d, j):
        return remote(sb.at[d, j], rb.at[d, j], c_send.at[d, j], c_recv.at[d, j], v, chain_to(d))

    def scale_copy(d, j):
        return remote(qs.at[d, j], qr.at[d, j], q_send.at[d, j], q_recv.at[d, j], v, chain_to(d))

    def head_copy(d, a):
        return remote(hs.at[d, a], hr.at[d, a], h_send.at[d, a], h_recv.at[d, a], v, chain_to(d))

    def head(d, a, pos):
        @pl.when(pos > 0)
        def _():
            head_copy(d, a).wait_recv()

        own, sib, up = srow[a], ssib[a], hr[d, a]
        new = own + sib + up
        hs[d, a] = new

        @pl.when(pos < CHAIN - 1)
        def _():
            head_copy(d, a).start()

        inverse = 1.0 / new
        factors = [jnp.sqrt(part * inverse) for part in (own, sib, up)]
        for m, depth in enumerate((D_DRAFT, D_TARGET)):
            grow_by = jnp.where(pos == CHAIN - 1, math.sqrt(depth), 1.0)
            pick = lane == sub + (m * HALF + d * 2 * BLOCK) + core * BLOCK
            for n, factor in enumerate(factors):
                column = jnp.sum(jnp.where(pick, factor, 0.0), axis=1, keepdims=True)
                fb[d, a, m, n] = jnp.broadcast_to(column * grow_by, (BLOCK, 128))

    def chain(d, s):
        pos = chip if d else (CHAIN - 1) - chip
        j = s - LAG - pos * HOP
        groups = CW // 128

        def cut(g):
            return slice(g * 128, (g + 1) * 128)

        @pl.when((j >= 0) & (j < CHUNKS))
        def _():
            a = j // PER_STAGE
            r = j % PER_STAGE
            m = r % 2

            @pl.when(r == 0)
            def _():
                head(d, a, pos)

            def local_sum():
                fo, fs = fb[d, a, m, 0], fb[d, a, m, 1]
                return [
                    pb[j, core, d, :, cut(g)] * fo + pr[j, d, :, cut(g)] * fs
                    for g in range(groups)
                ]

            def with_received():
                chunk_copy(d, j).wait_recv()
                scale_copy(d, j).wait_recv()
                fu = fb[d, a, m, 2] * qr[d, j]
                return [
                    part + rb[d, j, :, cut(g)].astype(F32) * fu
                    for g, part in enumerate(local_sum())
                ]

            def send(parts):
                top = functools.reduce(jnp.maximum, [jnp.abs(p) for p in parts])
                top = jnp.maximum(jnp.max(top, axis=0, keepdims=True), 1e-30)
                up = LEVELS / top
                qs[d, j] = top * (1.0 / LEVELS)
                for g, part in enumerate(parts):
                    sb[d, j, :, cut(g)] = (
                        jnp.round(part * up).astype(jnp.int32).astype(jnp.int16)
                    )
                scale_copy(d, j).start()
                chunk_copy(d, j).start()

            @pl.when(pos == 0)
            def _():
                send(local_sum())

            @pl.when((pos > 0) & (pos < CHAIN - 1))
            def _():
                send(with_received())

            @pl.when(pos == CHAIN - 1)
            def _():
                logits = with_received()
                base = (r // 2) * CW
                bits, tok = bt[a, 0], bt[a, 1]
                at = a * 2 + m
                high, summed, picked = st[at, 0], st[at, 1], st[at, 2]
                masked, keeps = [], []
                for g in range(groups):
                    off = pl.ds(pl.multiple_of(base + g * 128, 128), 128)
                    chosen = colid[:, off] == tok
                    keep = ((bits >> cls[:, off]) & 1 == 1) | chosen
                    picked = picked + jnp.where(chosen, logits[g], 0.0)
                    masked.append(jnp.where(keep, logits[g], NEG))
                    keeps.append(keep)
                top = functools.reduce(jnp.maximum, masked, high)
                summed = summed * jnp.exp(high - top)
                for g in range(groups):
                    summed = summed + jnp.where(keeps[g], jnp.exp(masked[g] - top), 0.0)
                st[at, 0] = top
                st[at, 1] = summed
                st[at, 2] = picked

    def slot(s, carry):
        @pl.when(s == 0)
        def _():
            prepare(0)

        @pl.when(s == PER_STAGE)
        def _():
            prepare(1)

        @pl.when(s < CHUNKS)
        def _():
            multiply(s)
            d2_copy(s).start()

        late = s - LAG

        @pl.when((late >= 0) & (late < CHUNKS))
        def _():
            d2_copy(late).wait_recv()

            @pl.when(late % PER_STAGE == 0)
            def _():
                a = late // PER_STAGE
                remote(
                    srow.at[a], ssib.at[a], sib_send.at[a], sib_recv.at[a], v, mate
                ).wait_recv()

        chain(1, s)
        chain(0, s)
        return carry

    lax.fori_loop(0, CHUNKS + LAG + (CHAIN - 1) * HOP, slot, 0)

    owner = (chip == 0) | (chip == CHAIN - 1)
    lane1 = lax.broadcasted_iota(jnp.int32, (1, 128), 1)

    def merge(rows):
        sums = jnp.sum(rows, axis=0, keepdims=True)
        top = jnp.max(rows, axis=0, keepdims=True)
        lse = top + jnp.log(jnp.sum(jnp.exp(rows - top), axis=0, keepdims=True))
        return jnp.where(lane1 < 64, lse, sums)

    def fin_copy(t):
        return remote(
            grow.at[0], gall.at[place], fin_send.at[t], fin_recv.at[place],
            half * PLANE + (place + t) % PLANE, b,
        )

    def z_copy(n):
        hh = (half + n % 2) % 2
        end = chip // 2
        low = end * 3
        other = 2 - end
        target = low if n < 2 else other
        return remote(
            zrow.at[0], zall.at[half], z_send.at[n], z_recv.at[half],
            hh * PLANE + place, target * 2 + core,
        )

    def z_arrived(hh):
        remote(
            zrow.at[0], zall.at[hh], z_send.at[0], z_recv.at[hh], v, b
        ).wait_recv()

    @pl.when(owner)
    def _():
        total = jnp.zeros((BLOCK, 128), F32)
        for a in range(2):
            stage = half if a == 0 else 1 - half
            for m in range(2):
                high, summed, picked = (st[a * 2 + m, n] for n in range(3))
                top = jnp.max(high, axis=1, keepdims=True)
                mass = jnp.sum(summed * jnp.exp(high - top), axis=1, keepdims=True)
                lse = jnp.where(mass > 0.0, top + jnp.log(jnp.maximum(mass, 1e-37)), NEG)
                pick = jnp.sum(picked, axis=1, keepdims=True)
                at = sub + stage * BLOCK + m * 32
                total = total + jnp.where(lane == at, lse, 0.0)
                total = total + jnp.where(lane == at + 64, pick, 0.0)
        row = jnp.sum(total, axis=0, keepdims=True)
        grow[0] = row
        gall[place] = row

        def start(t, carry):
            fin_copy(t).start()
            return carry

        lax.fori_loop(1, PLANE, start, 0)

        def wait(t, carry):
            n = (place + t) % PLANE
            remote(
                grow.at[0], gall.at[n], fin_send.at[t], fin_recv.at[n], v, b
            ).wait_recv()
            return carry

        lax.fori_loop(1, PLANE, wait, 0)
        row = merge(gall[...].reshape(PLANE, 128))
        zrow[0] = row
        zall[half] = row
        for n in (3, 2, 1):
            z_copy(n).start()
        z_arrived(1 - half)

    @pl.when(jnp.logical_not(owner))
    def _():
        z_arrived(0)
        z_arrived(1)

    row = merge(zall[...].reshape(2, 128))
    stage = chip // 2

    def part(n):
        return jnp.where(
            stage == 0, row[:, n * 32 : n * 32 + 16], row[:, n * 32 + 16 : n * 32 + 32]
        )

    logprob = part(3) - part(1)
    logprob_ref[...] = logprob
    ratio_ref[...] = logprob - (part(2) - part(0))

    to_partner.wait_send()

    def drain_gather(t, carry):
        near_copy(t).wait_send()
        far_copy(t).wait_send()
        return carry

    lax.fori_loop(1, PLANE, drain_gather, 0)
    for a in range(2):
        remote(srow.at[a], ssib.at[a], sib_send.at[a], sib_recv.at[a], v, mate).wait_send()

    def drain_chunks(j, carry):
        d2_copy(j).wait_send()
        return carry

    lax.fori_loop(0, CHUNKS, drain_chunks, 0)
    for d in range(2):
        pos = chip if d else (CHAIN - 1) - chip

        @pl.when(pos < CHAIN - 1)
        def _():
            for a in range(2):
                head_copy(d, a).wait_send()

            def drain_chain(j, carry):
                chunk_copy(d, j).wait_send()
                scale_copy(d, j).wait_send()
                return carry

            lax.fori_loop(0, CHUNKS, drain_chain, 0)

    @pl.when(owner)
    def _():
        def drain_final(t, carry):
            fin_copy(t).wait_send()
            return carry

        lax.fori_loop(1, PLANE, drain_final, 0)
        for n in (3, 2, 1):
            z_copy(n).wait_send()


def shards(
    draft_hidden, target_hidden, draft_gain, target_gain, draft_head, target_head,
    token_class, grammar_bits, draft_tokens,
):
    kd, width = draft_head.shape
    kt = target_head.shape[0]
    kk = kd + kt
    vmem, dma = pltpu.VMEM, pltpu.SemaphoreType.DMA
    i32, i16 = jnp.int32, jnp.int16
    scratch = [
        vmem((2 * PLANE, 4, kk), BF16),
        vmem((1, kk), F32),
        vmem((Q * CW, kd), BF16),
        vmem((Q * CW, kt), BF16),
        vmem((1, width), i32),
        vmem((1, Q * CW), i32),
        vmem((1, Q * CW), i32),
        pltpu.SMEM((ROWS,), i32),
        pltpu.SMEM((ROWS,), i32),
        vmem((HALF, kk), F32),
        vmem((2, HALF, kk), BF16),
        vmem((2, 1, 128), F32),
        vmem((2, 1, 128), F32),
        vmem((CHUNKS, 2, 2, BLOCK, CW), F32),
        vmem((CHUNKS, 2, BLOCK, CW), F32),
        vmem((2, CHUNKS, BLOCK, CW), i16),
        vmem((2, CHUNKS, BLOCK, CW), i16),
        vmem((2, CHUNKS, 1, 128), F32),
        vmem((2, CHUNKS, 1, 128), F32),
        vmem((2, 2, 1, 128), F32),
        vmem((2, 2, 1, 128), F32),
        vmem((2, 2, 2, 3, BLOCK, 128), F32),
        vmem((2, 2, BLOCK, 128), i32),
        vmem((4, 3, BLOCK, 128), F32),
        vmem((1, 1, 128), F32),
        vmem((PLANE, 1, 128), F32),
        vmem((1, 1, 128), F32),
        vmem((2, 1, 128), F32),
        dma((7,)),
        dma((2 * pl.cdiv(width, WSPLIT),)),
        dma((PLANE,)),
        dma((PLANE,)),
        dma((1,)),
        dma((2 * PLANE,)),
        dma((CHUNKS,)),
        dma((CHUNKS,)),
        dma((2,)),
        dma((2,)),
        dma((2, CHUNKS)),
        dma((2, CHUNKS)),
        dma((2, CHUNKS)),
        dma((2, CHUNKS)),
        dma((2, 2)),
        dma((2, 2)),
        dma((PLANE,)),
        dma((PLANE,)),
        dma((4,)),
        dma((2,)),
    ]
    out = jax.ShapeDtypeStruct((1, BLOCK), F32)
    ratio, logprob = pl.pallas_call(
        functools.partial(kernel, (kd, kt, width)),
        out_shape=(out, out),
        in_specs=[pl.BlockSpec(memory_space=pl.ANY)] * 9,
        out_specs=(pl.BlockSpec(memory_space=pltpu.VMEM),) * 2,
        scratch_shapes=scratch,
        compiler_params=pltpu.CompilerParams(
            collective_id=0, has_side_effects=True, vmem_limit_bytes=62 * 1024 * 1024
        ),
        name="verify",
    )(
        draft_hidden,
        target_hidden,
        draft_gain.reshape(1, kd),
        target_gain.reshape(1, kt),
        draft_head.T,
        target_head.T,
        token_class.reshape(1, width),
        grammar_bits,
        draft_tokens,
    )
    return ratio.reshape(BLOCK), logprob.reshape(BLOCK)


def solution(mesh):
    in_specs = (
        P("vocab", "batch"),
        P("vocab", "batch"),
        P("batch"),
        P("batch"),
        P("batch", "vocab"),
        P("batch", "vocab"),
        P("vocab"),
        P(),
        P(),
    )
    out_specs = (P("batch"), P("batch"))
    return jax.shard_map(shards, mesh=mesh, in_specs=in_specs, out_specs=out_specs, check_vma=False)
```

time: 155 us -> 58.5 us (0.38)
  blocking collectives: 58.6 us -> 0 us
  Pallas kernels: 0 us -> 55.5 us
  waiting for transfers between devices: 49.9 us -> 0 us
  other arithmetic: 13.8 us -> 0 us
  between operations: 14.2 us -> 0.64 us
  local copies, waits for them, and re-layouts: 11.3 us -> 2.25 us
  matrix products: 6.15 us -> 0 us
    all_to_all x3 -> x0, blocking collectives: 58.6 us -> none  [sent_to_all(): lax.all_to_all(jnp.broadcast_to(value[None], (length, *value.shape)), axi...]
    pallas_call x0 -> x1, Pallas kernels: none -> 55.5 us  [shards(): pl.pallas_call(functools.partial(kernel, (kd, kt, width)), out_shape=(out...]
    unnamed x2 -> x0, waiting for transfers between devices: 49.9 us -> none
    unnamed x13 -> x2, local copies, waits for them, and re-layouts: 8.79 us -> 2.25 us
    dot_general x2 -> x0, matrix products: 6.15 us -> none  [the longest x1 4.9 us: shards(): jnp.dot(target_pieces, target_head, preferred_element_type=jnp.float32)]
    reduce_max x1 -> x0, other arithmetic: 4.74 us -> none  [shard_stats(): highest = jnp.max(masked, axis=1)]
    reduce_sum x4 -> x0, other arithmetic: 4.43 us -> none  [the longest x1 2.78 us: shard_stats(): picked = jnp.sum(jnp.where(chosen, logits, 0.0), axis=1)]
    concatenate x3 -> x0, other arithmetic: 2.28 us -> none  [the longest x1 2.19 us: sent_together_2(): both = jnp.concatenate(arrays, axis=along)]
  transfers between devices with their start and end apart: 1 -> 0, of which waited for: 1 -> 0; matrix products, arithmetic and copies ran while one was open for 0% -> 0% of each run, Pallas kernels for 0% -> 0%
where the time goes in v1:
time: 58.5 us; the launch traced here: 58.4 us
  Pallas kernels  55.5 us (95%)
  local copies, waits for them, and re-layouts  2.25 us (4%)
  between operations  0.64 us (1%)
    pallas_call x1, Pallas kernels, shards(): pl.pallas_call(functools.partial(kernel, (kd, kt, width)), out_shape=(out...  55.5 us
    unnamed x2, local copies, waits for them, and re-layouts  2.25 us

profile of v1, /device:TPU:8, one launch (start us, length us, event | category | flops | bytes accessed | tf_op | source)
XLA Modules:
  0.0 58.4 jit_solution(8666678364356087809)
XLA Ops:
  0.6 55.5 %verify.1 = (f32[1,16]{1,0:T(1,128)}, f32[1,16]{1,0:T(1,128)}) custom-call(bf16[4,512]{1,0:T(4,128)(2,1)} %dh.1, bf16[4,1024]{1,0:T(4,128)(2,1)} %th.1, f32[1,512]{1,0:T(1,128)} %bitcast.11, f32[1,1024]{1,0:T(1,128)} %bitcast.10, bf16[4008,512]{1,0:T(8,128)(2,1)} %bitcast.8, bf16[4008,1024]{1,0:T(8,128)(2,1)} %bitcast.7, s32[1,4008]{1,0:T(1,128)} %bitcast.9, ...), custom_call_target="tpu_custom_call" | custom-call | tf_op jit(solution)/shard_map/verify/pallas_call | solution.py:559
  56.1 1.1 %copy.13 = f32[16]{0:T(128)} copy(f32[16]{0:T(128)} %bitcast.13) | data formatting | bytes 128
  57.2 1.1 %copy.14 = f32[16]{0:T(128)} copy(f32[16]{0:T(128)} %bitcast.12) | data formatting | bytes 128

commit v2 on v1

v2 whole, which is shorter than its diff:
```python
import functools

import jax
import jax.numpy as jnp
from jax import lax
from jax.experimental import pallas as pl
from jax.experimental.pallas import tpu as pltpu
from jax.sharding import PartitionSpec as P

D_DRAFT = 4096
D_TARGET = 8192
EPS = 1e-05
NEG = -1e30
F32 = jnp.float32
BF16 = jnp.bfloat16

PLANE = 16
CHAIN = 4
LINE = 16
ROWS = 128
SHARE = 4
BLOCK = 16
MINE = 32
CW = 256
CHUNKS = 16
LAG = 2
HOP = 4
WSPLIT = 1024
LEVELS = 32760.0


def kernel(
    dims,
    dh, th, dg, tg, wd_hbm, wt_hbm, cls_hbm, bits_hbm, tok_hbm,
    out_ref,
    own, other, gain, sums, xg, wd, wt, cls_in, cls, colid, bits_s, tok_s,
    xf, xn, pb, pr, sb, rb, qs, qr, bt, st,
    grow, gall, zrow, zall,
    load_sem, w_sem, sum_send, sum_recv, pair_send, pair_recv,
    near_send, far_send, g_recv, d2_send, d2_recv,
    c_send, c_recv, q_send, q_recv,
    fin_send, fin_recv, z_send, z_recv,
):
    kd, kt, width = dims
    kk = kd + kt
    v = lax.axis_index("vocab")
    b = lax.axis_index("batch")
    half = v // PLANE
    place = v % PLANE
    chip = b // 2
    core = b % 2
    mate = chip * 2 + (1 - core)
    partner = (v + PLANE) % (2 * PLANE)
    here = half * 8 + b

    def remote(src, dst, send, recv, vv, bb):
        return pltpu.make_async_remote_copy(
            src_ref=src, dst_ref=dst, send_sem=send, recv_sem=recv,
            device_id=(vv, bb), device_id_type=pl.DeviceIdType.MESH,
        )

    barrier = pltpu.get_barrier_semaphore()

    def greet(vv, bb):
        pl.semaphore_signal(
            barrier, inc=1, device_id=(vv, bb), device_id_type=pl.DeviceIdType.MESH
        )

    def greet_line(t, carry):
        to = (here + t) % LINE
        greet((to // 8) * PLANE + place, to % 8)
        return carry

    def greet_plane(t, carry):
        greet(half * PLANE + (place + t) % PLANE, b)
        return carry

    lax.fori_loop(1, LINE, greet_line, 0)
    lax.fori_loop(1, PLANE, greet_plane, 0)

    loads = [
        pltpu.make_async_copy(dh, own.at[:, 0:kd], load_sem.at[0]),
        pltpu.make_async_copy(th, own.at[:, kd:kk], load_sem.at[1]),
        pltpu.make_async_copy(dg, gain.at[:, 0:kd], load_sem.at[2]),
        pltpu.make_async_copy(tg, gain.at[:, kd:kk], load_sem.at[3]),
        pltpu.make_async_copy(cls_hbm, cls_in, load_sem.at[4]),
        pltpu.make_async_copy(bits_hbm, bits_s, load_sem.at[5]),
        pltpu.make_async_copy(tok_hbm, tok_s, load_sem.at[6]),
    ]
    for copy in loads:
        copy.start()
    weights = []
    for hbm, ref in ((wd_hbm, wd), (wt_hbm, wt)):
        for at in range(0, width, WSPLIT):
            rows = pl.ds(at, min(WSPLIT, width - at))
            weights.append((hbm.at[rows], ref.at[rows]))
    weights = [
        pltpu.make_async_copy(src, dst, w_sem.at[n]) for n, (src, dst) in enumerate(weights)
    ]
    for copy in weights:
        copy.start()

    lane4 = lax.broadcasted_iota(jnp.int32, (SHARE, 128), 1)
    sub4 = lax.broadcasted_iota(jnp.int32, (SHARE, 128), 0)
    models = ((0, kd, D_DRAFT), (kd, kk, D_TARGET))
    loads[0].wait()
    loads[1].wait()
    held = jnp.zeros((SHARE, 128), F32)
    for m, (lo, hi, _) in enumerate(models):
        part = own[:, lo:hi].astype(F32)
        square = jnp.sum(part * part, axis=1, keepdims=True)
        held = held + jnp.where(lane4 == sub4 + m * SHARE, square, 0.0)
    sums[here] = jnp.sum(held, axis=0, keepdims=True)

    pl.semaphore_wait(barrier, (LINE - 1) + (PLANE - 1))

    def pair_copy():
        return remote(own, other, pair_send.at[0], pair_recv.at[0], partner, b)

    def sum_copy(t):
        to = (here + t) % LINE
        return remote(
            sums.at[here], sums.at[here], sum_send.at[t], sum_recv.at[here],
            (to // 8) * PLANE + place, to % 8,
        )

    def sum_arrived(n):
        remote(sums.at[n], sums.at[n], sum_send.at[0], sum_recv.at[n], v, b).wait_recv()

    def start_sum(t, carry):
        sum_copy(t).start()
        return carry

    lax.fori_loop(1, LINE, start_sum, 0)
    pair_copy().start()

    for copy in loads[2:]:
        copy.wait()
    lane = lax.broadcasted_iota(jnp.int32, (MINE, 128), 1)
    sub = lax.broadcasted_iota(jnp.int32, (MINE, 128), 0)
    bits_col = jnp.zeros((MINE, 128), jnp.int32)
    tok_col = jnp.zeros((MINE, 128), jnp.int32)
    for stage in range(2):
        at = (stage * 4 + (chip // 2) * 2 + core) * BLOCK
        for r in range(BLOCK):
            row = sub == stage * BLOCK + r
            bits_col = jnp.where(row, bits_s[at + r], bits_col)
            tok_col = jnp.where(row, tok_s[at + r], tok_col)
    bt[0] = bits_col
    bt[1] = tok_col - v * width

    def normalise(rows, n, to):
        total = jnp.sum(sums[pl.ds(n * 8, 8)].reshape(8, 128), axis=0, keepdims=True)
        for m, (lo, hi, depth) in enumerate(models):
            column = jnp.sum(
                jnp.where(lane4 == sub4 + m * SHARE, total, 0.0), axis=1, keepdims=True
            )
            scale = lax.rsqrt(column / depth + EPS)
            xg[to, :, lo:hi] = (rows[:, lo:hi].astype(F32) * scale * gain[:, lo:hi]).astype(BF16)

    def near_copy(t):
        return remote(
            xg.at[v], xg.at[v], near_send.at[t], g_recv.at[v],
            half * PLANE + (place + t) % PLANE, b,
        )

    def far_copy(t):
        return remote(
            xg.at[partner], xg.at[partner], far_send.at[t], g_recv.at[partner],
            half * PLANE + (place + t) % PLANE, b,
        )

    def start_near(t, carry):
        near_copy(t).start()
        return carry

    def start_far(t, carry):
        far_copy(t).start()
        return carry

    def wait_same(t, carry):
        sum_arrived(half * 8 + (b + t) % 8)
        return carry

    def wait_opposite(t, carry):
        sum_arrived((1 - half) * 8 + t)
        return carry

    lax.fori_loop(1, 8, wait_same, 0)
    normalise(own, half, v)
    lax.fori_loop(1, PLANE, start_near, 0)
    lax.fori_loop(0, 8, wait_opposite, 0)
    pair_copy().wait_recv()
    normalise(other, 1 - half, partner)
    lax.fori_loop(1, PLANE, start_far, 0)

    lanes_all = lax.broadcasted_iota(jnp.int32, (1, CHUNKS * CW), 1)
    colid[...] = jnp.where(lanes_all < width, lanes_all, -(1 << 30))
    cls[...] = jnp.full((1, CHUNKS * CW), 30, jnp.int32)
    cls[:, 0:width] = cls_in[...]
    for m in range(2):
        st[m, 0] = jnp.full((MINE, 128), NEG, F32)
        st[m, 1] = jnp.zeros((MINE, 128), F32)
        st[m, 2] = jnp.zeros((MINE, 128), F32)
    for copy in weights:
        copy.wait()
    wd[width:, :] = jnp.zeros((CHUNKS * CW - width, kd), BF16)
    wt[width:, :] = jnp.zeros((CHUNKS * CW - width, kt), BF16)

    def settle(stage, first):
        def wait_row(t, carry):
            n = stage * PLANE + (place + t) % PLANE
            remote(xg.at[n], xg.at[n], near_send.at[0], g_recv.at[n], v, b).wait_recv()
            return carry

        lax.fori_loop(1, PLANE, wait_row, 0)

        def unpack(i, carry):
            for k in range(4):
                xf[i, 4 * k : 4 * k + 4, :] = xg[stage * PLANE + 4 * i + k].astype(F32)
            at = pl.multiple_of((stage * 4 + i) * BLOCK, BLOCK)
            xn[pl.ds(at, BLOCK), :] = xf[i].astype(BF16)
            return carry

        lax.fori_loop(0, 4, unpack, 0)

    settle(half, True)
    settle(1 - half, False)

    def multiply(s):
        for m, ref in enumerate((wd, wt)):
            lo, hi, _ = models[m]
            for n in range(CW // 256):
                at = pl.multiple_of(s * CW + n * 256, 256)
                out = lax.dot_general(
                    xn[:, lo:hi], ref[pl.ds(at, 256), :], (((1,), (1,)), ((), ())),
                    preferred_element_type=F32,
                )
                col = m * CW + n * 256
                for blk in range(ROWS // BLOCK):
                    row = (blk // 4) * BLOCK
                    pb[s, blk % 2, (blk // 2) % 2, row : row + BLOCK, col : col + 256] = out[
                        blk * BLOCK : (blk + 1) * BLOCK
                    ]

    def d2_copy(j):
        return remote(pb.at[j, 1 - core], pr.at[j], d2_send.at[j], d2_recv.at[j], v, mate)

    def chain_to(d):
        return (chip + (1 if d else -1)) * 2 + core

    def chunk_copy(d, j):
        return remote(sb.at[d, j], rb.at[d, j], c_send.at[d, j], c_recv.at[d, j], v, chain_to(d))

    def scale_copy(d, j):
        return remote(qs.at[d, j], qr.at[d, j], q_send.at[d, j], q_recv.at[d, j], v, chain_to(d))

    groups = CW // 128

    def cut(m, g):
        at = m * CW + g * 128
        return slice(at, at + 128)

    def chain(d, s):
        pos = chip if d else (CHAIN - 1) - chip
        j = s - LAG - pos * HOP

        @pl.when((j >= 0) & (j < CHUNKS))
        def _():
            def local_sum(m):
                return [
                    pb[j, core, d, :, cut(m, g)] + pr[j, d, :, cut(m, g)] for g in range(groups)
                ]

            def wait_received():
                chunk_copy(d, j).wait_recv()
                scale_copy(d, j).wait_recv()

            def with_received(m):
                unit = qr[d, j, :, m * 128 : (m + 1) * 128]
                return [
                    part + rb[d, j, :, cut(m, g)].astype(F32) * unit
                    for g, part in enumerate(local_sum(m))
                ]

            def code(m, parts):
                top = functools.reduce(jnp.maximum, [jnp.abs(p) for p in parts])
                top = jnp.maximum(jnp.max(top, axis=0, keepdims=True), 1e-30)
                up = LEVELS / top
                qs[d, j, :, m * 128 : (m + 1) * 128] = top * (1.0 / LEVELS)
                for g, part in enumerate(parts):
                    sb[d, j, :, cut(m, g)] = (
                        jnp.round(part * up).astype(jnp.int32).astype(jnp.int16)
                    )

            def send():
                scale_copy(d, j).start()
                chunk_copy(d, j).start()

            @pl.when(pos == 0)
            def _():
                for m in range(2):
                    code(m, local_sum(m))
                send()

            @pl.when((pos > 0) & (pos < CHAIN - 1))
            def _():
                wait_received()
                for m in range(2):
                    code(m, with_received(m))
                send()

            @pl.when(pos == CHAIN - 1)
            def _():
                wait_received()
                bits, tok = bt[0], bt[1]
                for m in range(2):
                    logits = with_received(m)
                    high, summed, picked = st[m, 0], st[m, 1], st[m, 2]
                    masked, keeps = [], []
                    for g in range(groups):
                        off = pl.ds(pl.multiple_of(j * CW + g * 128, 128), 128)
                        chosen = colid[:, off] == tok
                        keep = ((bits >> cls[:, off]) & 1 == 1) | chosen
                        picked = picked + jnp.where(chosen, logits[g], 0.0)
                        masked.append(jnp.where(keep, logits[g], NEG))
                        keeps.append(keep)
                    top = functools.reduce(jnp.maximum, masked, high)
                    summed = summed * jnp.exp(high - top)
                    for g in range(groups):
                        summed = summed + jnp.where(keeps[g], jnp.exp(masked[g] - top), 0.0)
                    st[m, 0] = top
                    st[m, 1] = summed
                    st[m, 2] = picked

    def slot(s, carry):
        @pl.when(s < CHUNKS)
        def _():
            multiply(s)
            d2_copy(s).start()

        late = s - LAG

        @pl.when((late >= 0) & (late < CHUNKS))
        def _():
            d2_copy(late).wait_recv()

        chain(1, s)
        chain(0, s)
        return carry

    lax.fori_loop(0, CHUNKS + LAG + (CHAIN - 1) * HOP, slot, 0)

    owner = (chip == 0) | (chip == CHAIN - 1)
    lane1 = lax.broadcasted_iota(jnp.int32, (1, 128), 1)

    def merge(rows):
        total = jnp.sum(rows, axis=0, keepdims=True)
        top = jnp.max(rows, axis=0, keepdims=True)
        lse = top + jnp.log(jnp.sum(jnp.exp(rows - top), axis=0, keepdims=True))
        return jnp.where(lane1 < 64, lse, total)

    def fin_copy(t):
        return remote(
            grow.at[0], gall.at[place], fin_send.at[t], fin_recv.at[place],
            half * PLANE + (place + t) % PLANE, b,
        )

    def z_copy(n):
        hh = (half + n % 2) % 2
        end = chip // 2
        target = end * 3 if n < 2 else 2 - end
        return remote(
            zrow.at[0], zall.at[half], z_send.at[n], z_recv.at[half],
            hh * PLANE + place, target * 2 + core,
        )

    def z_arrived(hh):
        remote(zrow.at[0], zall.at[hh], z_send.at[0], z_recv.at[hh], v, b).wait_recv()

    @pl.when(owner)
    def _():
        total = jnp.zeros((MINE, 128), F32)
        for m in range(2):
            high, summed, picked = (st[m, n] for n in range(3))
            top = jnp.max(high, axis=1, keepdims=True)
            mass = jnp.sum(summed * jnp.exp(high - top), axis=1, keepdims=True)
            lse = jnp.where(mass > 0.0, top + jnp.log(jnp.maximum(mass, 1e-37)), NEG)
            pick = jnp.sum(picked, axis=1, keepdims=True)
            total = total + jnp.where(lane == sub + m * 32, lse, 0.0)
            total = total + jnp.where(lane == sub + m * 32 + 64, pick, 0.0)
        row = jnp.sum(total, axis=0, keepdims=True)
        grow[0] = row
        gall[place] = row

        def start(t, carry):
            fin_copy(t).start()
            return carry

        lax.fori_loop(1, PLANE, start, 0)

        def wait(t, carry):
            n = (place + t) % PLANE
            remote(grow.at[0], gall.at[n], fin_send.at[0], fin_recv.at[n], v, b).wait_recv()
            return carry

        lax.fori_loop(1, PLANE, wait, 0)
        row = merge(gall[...].reshape(PLANE, 128))
        zrow[0] = row
        zall[half] = row
        for n in (3, 1, 2):
            z_copy(n).start()
        z_arrived(1 - half)

    @pl.when(jnp.logical_not(owner))
    def _():
        z_arrived(0)
        z_arrived(1)

    row = merge(zall[...].reshape(2, 128))
    for n in range(4):
        out_ref[n : n + 1, :] = jnp.where(
            chip // 2 == 0, row[:, n * 32 : n * 32 + 16], row[:, n * 32 + 16 : n * 32 + 32]
        )

    pair_copy().wait_send()

    def drain_gather(t, carry):
        sum_copy(t).wait_send()
        near_copy(t).wait_send()
        far_copy(t).wait_send()
        return carry

    lax.fori_loop(1, PLANE, drain_gather, 0)

    def drain_chunks(j, carry):
        d2_copy(j).wait_send()
        return carry

    lax.fori_loop(0, CHUNKS, drain_chunks, 0)
    for d in range(2):
        pos = chip if d else (CHAIN - 1) - chip

        @pl.when(pos < CHAIN - 1)
        def _():
            def drain_chain(j, carry):
                chunk_copy(d, j).wait_send()
                scale_copy(d, j).wait_send()
                return carry

            lax.fori_loop(0, CHUNKS, drain_chain, 0)

    @pl.when(owner)
    def _():
        def drain_final(t, carry):
            fin_copy(t).wait_send()
            return carry

        lax.fori_loop(1, PLANE, drain_final, 0)
        for n in (3, 1, 2):
            z_copy(n).wait_send()


def shards(
    draft_hidden, target_hidden, draft_gain, target_gain, draft_head, target_head,
    token_class, grammar_bits, draft_tokens,
):
    kd, width = draft_head.shape
    kt = target_head.shape[0]
    kk = kd + kt
    vmem, dma = pltpu.VMEM, pltpu.SemaphoreType.DMA
    i32, i16 = jnp.int32, jnp.int16
    scratch = [
        vmem((SHARE, kk), BF16),
        vmem((SHARE, kk), BF16),
        vmem((1, kk), F32),
        vmem((LINE, 1, 128), F32),
        vmem((2 * PLANE, SHARE, kk), BF16),
        vmem((CHUNKS * CW, kd), BF16),
        vmem((CHUNKS * CW, kt), BF16),
        vmem((1, width), i32),
        vmem((1, CHUNKS * CW), i32),
        vmem((1, CHUNKS * CW), i32),
        pltpu.SMEM((ROWS,), i32),
        pltpu.SMEM((ROWS,), i32),
        vmem((4, BLOCK, kk), F32),
        vmem((ROWS, kk), BF16),
        vmem((CHUNKS, 2, 2, MINE, 2 * CW), F32),
        vmem((CHUNKS, 2, MINE, 2 * CW), F32),
        vmem((2, CHUNKS, MINE, 2 * CW), i16),
        vmem((2, CHUNKS, MINE, 2 * CW), i16),
        vmem((2, CHUNKS, 1, 256), F32),
        vmem((2, CHUNKS, 1, 256), F32),
        vmem((2, MINE, 128), i32),
        vmem((2, 3, MINE, 128), F32),
        vmem((1, 1, 128), F32),
        vmem((PLANE, 1, 128), F32),
        vmem((1, 1, 128), F32),
        vmem((2, 1, 128), F32),
        dma((7,)),
        dma((2 * pl.cdiv(width, WSPLIT),)),
        dma((LINE,)),
        dma((LINE,)),
        dma((1,)),
        dma((1,)),
        dma((PLANE,)),
        dma((PLANE,)),
        dma((2 * PLANE,)),
        dma((CHUNKS,)),
        dma((CHUNKS,)),
        dma((2, CHUNKS)),
        dma((2, CHUNKS)),
        dma((2, CHUNKS)),
        dma((2, CHUNKS)),
        dma((PLANE,)),
        dma((PLANE,)),
        dma((4,)),
        dma((2,)),
    ]
    parts = pl.pallas_call(
        functools.partial(kernel, (kd, kt, width)),
        out_shape=jax.ShapeDtypeStruct((4, BLOCK), F32),
        in_specs=[pl.BlockSpec(memory_space=pl.ANY)] * 9,
        out_specs=pl.BlockSpec(memory_space=pltpu.VMEM),
        scratch_shapes=scratch,
        compiler_params=pltpu.CompilerParams(
            collective_id=0, has_side_effects=True, vmem_limit_bytes=62 * 1024 * 1024
        ),
        name="verify",
    )(
        draft_hidden,
        target_hidden,
        draft_gain.reshape(1, kd),
        target_gain.reshape(1, kt),
        draft_head.T,
        target_head.T,
        token_class.reshape(1, width),
        grammar_bits,
        draft_tokens,
    )
    draft_lse, target_lse, draft_pick, target_pick = (parts[n] for n in range(4))
    logprob = target_pick - target_lse
    return logprob - (draft_pick - draft_lse), logprob


def solution(mesh):
    in_specs = (
        P("vocab", "batch"),
        P("vocab", "batch"),
        P("batch"),
        P("batch"),
        P("batch", "vocab"),
        P("batch", "vocab"),
        P("vocab"),
        P(),
        P(),
    )
    out_specs = (P("batch"), P("batch"))
    return jax.shard_map(shards, mesh=mesh, in_specs=in_specs, out_specs=out_specs, check_vma=False)
```

time: 58.5 us -> 58.6 us (level)
  local copies, waits for them, and re-layouts: 2.25 us -> 0 us
  other arithmetic: 0 us -> 1.35 us
  Pallas kernels: 55.5 us -> 56.5 us
    unnamed x2 -> x0, local copies, waits for them, and re-layouts: 2.25 us -> none
    sub x0 -> x1, other arithmetic: none -> 1.35 us  [shards(): return (logprob - (draft_pick - draft_lse), logprob)]
    pallas_call x1, Pallas kernels: 55.5 us -> 56.5 us  [shards(): pl.pallas_call(functools.partial(kernel, (kd, kt, width)), out_shape=jax....]
where the time goes in v2:
time: 58.6 us; the launch traced here: 58.5 us
  Pallas kernels  56.5 us (96%)
  other arithmetic  1.35 us (2%)
  between operations  0.64 us (1%)
    pallas_call x1, Pallas kernels, shards(): pl.pallas_call(functools.partial(kernel, (kd, kt, width)), out_shape=jax....  56.5 us
    sub x1, other arithmetic, shards(): return (logprob - (draft_pick - draft_lse), logprob)  1.35 us

profile of v2, /device:TPU:8, one launch (start us, length us, event | category | flops | bytes accessed | tf_op | source)
XLA Modules:
  0.0 58.5 jit_solution(2332485196747279967)
XLA Ops:
  0.6 56.5 %verify.1 = f32[4,16]{1,0:T(4,128)} custom-call(bf16[4,512]{1,0:T(4,128)(2,1)} %dh.1, bf16[4,1024]{1,0:T(4,128)(2,1)} %th.1, f32[1,512]{1,0:T(1,128)} %bitcast.14, f32[1,1024]{1,0:T(1,128)} %bitcast.13, bf16[4008,512]{1,0:T(8,128)(2,1)} %bitcast.11, bf16[4008,1024]{1,0:T(8,128)(2,1)} %bitcast.10, s32[1,4008]{1,0:T(1,128)} %bitcast.12, s32[128]{0:T(128)} %bits_hbm.1, ...), custom_call_target="tpu_custom_call" | custom-call | tf_op jit(solution)/shard_map/verify/pallas_call | solution.py:520
  57.2 1.3 %bitcast_subtract_fusion = (f32[16]{0:T(128)}, f32[16]{0:T(128)}) fusion(f32[4,16]{1,0:T(4,128)} %verify.1), kind=kLoop, calls=%fused_computation | loop fusion | flops 48 | bytes 384 | tf_op jit(solution)/shard_map/sub | solution.py:543

commit v3 on v2

--- a/solution.py
+++ b/solution.py
@@ -277,21 +277,22 @@
                 scale_copy(d, j).wait_recv()
 
             def with_received(m):
-                unit = qr[d, j, :, m * 128 : (m + 1) * 128]
+                unit = qr[d, j]
                 return [
                     part + rb[d, j, :, cut(m, g)].astype(F32) * unit
                     for g, part in enumerate(local_sum(m))
                 ]
 
-            def code(m, parts):
-                top = functools.reduce(jnp.maximum, [jnp.abs(p) for p in parts])
+            def code(parts):
+                top = functools.reduce(jnp.maximum, [jnp.abs(p) for p in sum(parts, [])])
                 top = jnp.maximum(jnp.max(top, axis=0, keepdims=True), 1e-30)
                 up = LEVELS / top
-                qs[d, j, :, m * 128 : (m + 1) * 128] = top * (1.0 / LEVELS)
-                for g, part in enumerate(parts):
-                    sb[d, j, :, cut(m, g)] = (
-                        jnp.round(part * up).astype(jnp.int32).astype(jnp.int16)
-                    )
+                qs[d, j] = top * (1.0 / LEVELS)
+                for m in range(2):
+                    for g, part in enumerate(parts[m]):
+                        sb[d, j, :, cut(m, g)] = (
+                            jnp.round(part * up).astype(jnp.int32).astype(jnp.int16)
+                        )
 
             def send():
                 scale_copy(d, j).start()
@@ -299,15 +300,13 @@
 
             @pl.when(pos == 0)
             def _():
-                for m in range(2):
-                    code(m, local_sum(m))
+                code([local_sum(m) for m in range(2)])
                 send()
 
             @pl.when((pos > 0) & (pos < CHAIN - 1))
             def _():
                 wait_received()
-                for m in range(2):
-                    code(m, with_received(m))
+                code([with_received(m) for m in range(2)])
                 send()
 
             @pl.when(pos == CHAIN - 1)
@@ -378,6 +377,34 @@
     def z_arrived(hh):
         remote(zrow.at[0], zall.at[hh], z_send.at[0], z_recv.at[hh], v, b).wait_recv()
 
+    def drain():
+        pair_copy().wait_send()
+
+        def drain_gather(t, carry):
+            sum_copy(t).wait_send()
+            near_copy(t).wait_send()
+            far_copy(t).wait_send()
+            return carry
+
+        lax.fori_loop(1, PLANE, drain_gather, 0)
+
+        def drain_chunks(j, carry):
+            d2_copy(j).wait_send()
+            return carry
+
+        lax.fori_loop(0, CHUNKS, drain_chunks, 0)
+        for d in range(2):
+            pos = chip if d else (CHAIN - 1) - chip
+
+            @pl.when(pos < CHAIN - 1)
+            def _():
+                def drain_chain(j, carry):
+                    chunk_copy(d, j).wait_send()
+                    scale_copy(d, j).wait_send()
+                    return carry
+
+                lax.fori_loop(0, CHUNKS, drain_chain, 0)
+
     @pl.when(owner)
     def _():
         total = jnp.zeros((MINE, 128), F32)
@@ -398,6 +425,7 @@
             return carry
 
         lax.fori_loop(1, PLANE, start, 0)
+        drain()
 
         def wait(t, carry):
             n = (place + t) % PLANE
@@ -410,10 +438,19 @@
         zall[half] = row
         for n in (3, 1, 2):
             z_copy(n).start()
+
+        def drain_final(t, carry):
+            fin_copy(t).wait_send()
+            return carry
+
+        lax.fori_loop(1, PLANE, drain_final, 0)
+        for n in (3, 1, 2):
+            z_copy(n).wait_send()
         z_arrived(1 - half)
 
     @pl.when(jnp.logical_not(owner))
     def _():
+        drain()
         z_arrived(0)
         z_arrived(1)
 
@@ -422,43 +459,6 @@
         out_ref[n : n + 1, :] = jnp.where(
             chip // 2 == 0, row[:, n * 32 : n * 32 + 16], row[:, n * 32 + 16 : n * 32 + 32]
         )
-
-    pair_copy().wait_send()
-
-    def drain_gather(t, carry):
-        sum_copy(t).wait_send()
-        near_copy(t).wait_send()
-        far_copy(t).wait_send()
-        return carry
-
-    lax.fori_loop(1, PLANE, drain_gather, 0)
-
-    def drain_chunks(j, carry):
-        d2_copy(j).wait_send()
-        return carry
-
-    lax.fori_loop(0, CHUNKS, drain_chunks, 0)
-    for d in range(2):
-        pos = chip if d else (CHAIN - 1) - chip
-
-        @pl.when(pos < CHAIN - 1)
-        def _():
-            def drain_chain(j, carry):
-                chunk_copy(d, j).wait_send()
-                scale_copy(d, j).wait_send()
-                return carry
-
-            lax.fori_loop(0, CHUNKS, drain_chain, 0)
-
-    @pl.when(owner)
-    def _():
-        def drain_final(t, carry):
-            fin_copy(t).wait_send()
-            return carry
-
-        lax.fori_loop(1, PLANE, drain_final, 0)
-        for n in (3, 1, 2):
-            z_copy(n).wait_send()
 
 
 def shards(
@@ -489,8 +489,8 @@
         vmem((CHUNKS, 2, MINE, 2 * CW), F32),
         vmem((2, CHUNKS, MINE, 2 * CW), i16),
         vmem((2, CHUNKS, MINE, 2 * CW), i16),
-        vmem((2, CHUNKS, 1, 256), F32),
-        vmem((2, CHUNKS, 1, 256), F32),
+        vmem((2, CHUNKS, 1, 128), F32),
+        vmem((2, CHUNKS, 1, 128), F32),
         vmem((2, MINE, 128), i32),
         vmem((2, 3, MINE, 128), F32),
         vmem((1, 1, 128), F32),
@@ -519,7 +519,7 @@
     ]
     parts = pl.pallas_call(
         functools.partial(kernel, (kd, kt, width)),
-        out_shape=jax.ShapeDtypeStruct((4, BLOCK), F32),
+        out_shape=pltpu.VMEM((4, BLOCK), F32),
         in_specs=[pl.BlockSpec(memory_space=pl.ANY)] * 9,
         out_specs=pl.BlockSpec(memory_space=pltpu.VMEM),
         scratch_shapes=scratch,

time: 58.6 us -> 56.5 us (0.964)
  Pallas kernels: 56.5 us -> 55.3 us
  other arithmetic: 1.35 us -> 0.52 us
    pallas_call x1, Pallas kernels: 56.5 us -> 55.3 us  [shards(): pl.pallas_call(functools.partial(kernel, (kd, kt, width)), out_shape=pltp...]
    sub x1, other arithmetic: 1.35 us -> 0.52 us  [shards(): return (logprob - (draft_pick - draft_lse), logprob)]
where the time goes in v3:
time: 56.5 us
  Pallas kernels  55.3 us (98%)
  between operations  0.64 us (1%)
    pallas_call x1, Pallas kernels, shards(): pl.pallas_call(functools.partial(kernel, (kd, kt, width)), out_shape=pltp...  55.3 us

profile of v3, /device:TPU:8, one launch (start us, length us, event | category | flops | bytes accessed | tf_op | source)
XLA Modules:
  0.0 56.5 jit_solution(12343944859699216705)
XLA Ops:
  0.6 55.3 %verify.1 = f32[4,16]{1,0:T(4,128)S(1)} custom-call(bf16[4,512]{1,0:T(4,128)(2,1)} %dh.1, bf16[4,1024]{1,0:T(4,128)(2,1)} %th.1, f32[1,512]{1,0:T(1,128)} %bitcast.14, f32[1,1024]{1,0:T(1,128)} %bitcast.13, bf16[4008,512]{1,0:T(8,128)(2,1)} %bitcast.11, bf16[4008,1024]{1,0:T(8,128)(2,1)} %bitcast.10, s32[1,4008]{1,0:T(1,128)} %bitcast.12, s32[128]{0:T(128)} %bits_hbm.1, ...), custom_call_target="tpu_custom_call" | custom-call | tf_op jit(solution)/shard_map/verify/pallas_call | solution.py:520
  55.9 0.5 bitcast_subtract_fusion

commit v4 on v3

--- a/solution.py
+++ b/solution.py
@@ -15,6 +15,7 @@
 BF16 = jnp.bfloat16
 
 PLANE = 16
+AWAY = (10, 6, 9, 11, 14, 5, 7, 13, 2, 8, 15, 3, 1, 4, 12)
 CHAIN = 4
 LINE = 16
 ROWS = 128
@@ -66,17 +67,10 @@
             barrier, inc=1, device_id=(vv, bb), device_id_type=pl.DeviceIdType.MESH
         )
 
-    def greet_line(t, carry):
+    for t in AWAY:
+        greet(half * PLANE + (place + t) % PLANE, b)
         to = (here + t) % LINE
         greet((to // 8) * PLANE + place, to % 8)
-        return carry
-
-    def greet_plane(t, carry):
-        greet(half * PLANE + (place + t) % PLANE, b)
-        return carry
-
-    lax.fori_loop(1, LINE, greet_line, 0)
-    lax.fori_loop(1, PLANE, greet_plane, 0)
 
     loads = [
         pltpu.make_async_copy(dh, own.at[:, 0:kd], load_sem.at[0]),
@@ -131,8 +125,9 @@
         sum_copy(t).start()
         return carry
 
-    lax.fori_loop(1, LINE, start_sum, 0)
     pair_copy().start()
+    for t in (8, 9, 7, 10, 6, 11, 5, 12, 4, 13, 3, 14, 2, 15, 1):
+        sum_copy(t).start()
 
     for copy in loads[2:]:
         copy.wait()
@@ -141,7 +136,7 @@
     bits_col = jnp.zeros((MINE, 128), jnp.int32)
     tok_col = jnp.zeros((MINE, 128), jnp.int32)
     for stage in range(2):
-        at = (stage * 4 + (chip // 2) * 2 + core) * BLOCK
+        at = ((1 - chip // 2) * 4 + stage * 2 + core) * BLOCK
         for r in range(BLOCK):
             row = sub == stage * BLOCK + r
             bits_col = jnp.where(row, bits_s[at + r], bits_col)
@@ -188,11 +183,13 @@
 
     lax.fori_loop(1, 8, wait_same, 0)
     normalise(own, half, v)
-    lax.fori_loop(1, PLANE, start_near, 0)
+    for t in AWAY:
+        near_copy(t).start()
     lax.fori_loop(0, 8, wait_opposite, 0)
     pair_copy().wait_recv()
     normalise(other, 1 - half, partner)
-    lax.fori_loop(1, PLANE, start_far, 0)
+    for t in AWAY:
+        far_copy(t).start()
 
     lanes_all = lax.broadcasted_iota(jnp.int32, (1, CHUNKS * CW), 1)
     colid[...] = jnp.where(lanes_all < width, lanes_all, -(1 << 30))
@@ -238,8 +235,8 @@
                 )
                 col = m * CW + n * 256
                 for blk in range(ROWS // BLOCK):
-                    row = (blk // 4) * BLOCK
-                    pb[s, blk % 2, (blk // 2) % 2, row : row + BLOCK, col : col + 256] = out[
+                    row = (blk // 2) % 2 * BLOCK
+                    pb[s, blk % 2, 1 - blk // 4, row : row + BLOCK, col : col + 256] = out[
                         blk * BLOCK : (blk + 1) * BLOCK
                     ]
 
@@ -367,8 +364,7 @@
 
     def z_copy(n):
         hh = (half + n % 2) % 2
-        end = chip // 2
-        target = end * 3 if n < 2 else 2 - end
+        target = (1 - chip // 2) * 2 + n // 2
         return remote(
             zrow.at[0], zall.at[half], z_send.at[n], z_recv.at[half],
             hh * PLANE + place, target * 2 + core,
@@ -420,11 +416,8 @@
         grow[0] = row
         gall[place] = row
 
-        def start(t, carry):
+        for t in AWAY:
             fin_copy(t).start()
-            return carry
-
-        lax.fori_loop(1, PLANE, start, 0)
         drain()
 
         def wait(t, carry):
@@ -435,8 +428,7 @@
         lax.fori_loop(1, PLANE, wait, 0)
         row = merge(gall[...].reshape(PLANE, 128))
         zrow[0] = row
-        zall[half] = row
-        for n in (3, 1, 2):
+        for n in range(4):
             z_copy(n).start()
 
         def drain_final(t, carry):
@@ -444,20 +436,19 @@
             return carry
 
         lax.fori_loop(1, PLANE, drain_final, 0)
-        for n in (3, 1, 2):
+        for n in range(4):
             z_copy(n).wait_send()
-        z_arrived(1 - half)
 
     @pl.when(jnp.logical_not(owner))
     def _():
         drain()
-        z_arrived(0)
-        z_arrived(1)
-
+
+    z_arrived(0)
+    z_arrived(1)
     row = merge(zall[...].reshape(2, 128))
     for n in range(4):
         out_ref[n : n + 1, :] = jnp.where(
-            chip // 2 == 0, row[:, n * 32 : n * 32 + 16], row[:, n * 32 + 16 : n * 32 + 32]
+            chip % 2 == 0, row[:, n * 32 : n * 32 + 16], row[:, n * 32 + 16 : n * 32 + 32]
         )
 
 

time: 56.5 us -> 54.2 us (0.959)
  Pallas kernels: 55.3 us -> 52.7 us
    pallas_call x1, Pallas kernels: 55.3 us -> 52.7 us  [shards(): pl.pallas_call(functools.partial(kernel, (kd, kt, width)), out_shape=pltp...]
where the time goes in v4:
time: 54.2 us; the launch traced here: 53.8 us
  Pallas kernels  52.7 us (97%)
  between operations  0.64 us (1%)
    pallas_call x1, Pallas kernels, shards(): pl.pallas_call(functools.partial(kernel, (kd, kt, width)), out_shape=pltp...  52.7 us

profile of v4, /device:TPU:8, one launch (start us, length us, event | category | flops | bytes accessed | tf_op | source)
XLA Modules:
  0.0 53.8 jit_solution(7240050774312614652)
XLA Ops:
  0.6 52.7 %verify.1 = f32[4,16]{1,0:T(4,128)S(1)} custom-call(bf16[4,512]{1,0:T(4,128)(2,1)} %dh.1, bf16[4,1024]{1,0:T(4,128)(2,1)} %th.1, f32[1,512]{1,0:T(1,128)} %bitcast.14, f32[1,1024]{1,0:T(1,128)} %bitcast.13, bf16[4008,512]{1,0:T(8,128)(2,1)} %bitcast.11, bf16[4008,1024]{1,0:T(8,128)(2,1)} %bitcast.10, s32[1,4008]{1,0:T(1,128)} %bitcast.12, s32[128]{0:T(128)} %bits_hbm.1, ...), custom_call_target="tpu_custom_call" | custom-call | tf_op jit(solution)/shard_map/verify/pallas_call | solution.py:511
  53.3 0.5 bitcast_subtract_fusion

commit v5 on v4

--- a/solution.py
+++ b/solution.py
@@ -244,7 +244,7 @@
         return remote(pb.at[j, 1 - core], pr.at[j], d2_send.at[j], d2_recv.at[j], v, mate)
 
     def chain_to(d):
-        return (chip + (1 if d else -1)) * 2 + core
+        return (chip + 2 * d - 1) * 2 + core
 
     def chunk_copy(d, j):
         return remote(sb.at[d, j], rb.at[d, j], c_send.at[d, j], c_recv.at[d, j], v, chain_to(d))
@@ -258,8 +258,12 @@
         at = m * CW + g * 128
         return slice(at, at + 128)
 
-    def chain(d, s):
-        pos = chip if d else (CHAIN - 1) - chip
+    near_end = chip // 2
+    depth = chip + near_end * (CHAIN - 1 - 2 * chip)
+
+    def chain(ends_near, s):
+        d = near_end if ends_near else 1 - near_end
+        pos = (CHAIN - 1) - depth if ends_near else depth
         j = s - LAG - pos * HOP
 
         @pl.when((j >= 0) & (j < CHUNKS))
@@ -295,19 +299,16 @@
                 scale_copy(d, j).start()
                 chunk_copy(d, j).start()
 
-            @pl.when(pos == 0)
-            def _():
+            def first():
                 code([local_sum(m) for m in range(2)])
                 send()
 
-            @pl.when((pos > 0) & (pos < CHAIN - 1))
-            def _():
+            def middle():
                 wait_received()
                 code([with_received(m) for m in range(2)])
                 send()
 
-            @pl.when(pos == CHAIN - 1)
-            def _():
+            def last():
                 wait_received()
                 bits, tok = bt[0], bt[1]
                 for m in range(2):
@@ -329,6 +330,9 @@
                     st[m, 1] = summed
                     st[m, 2] = picked
 
+            pl.when(depth == 1)(middle)
+            pl.when(depth == 0)(last if ends_near else first)
+
     def slot(s, carry):
         @pl.when(s < CHUNKS)
         def _():
@@ -341,8 +345,8 @@
         def _():
             d2_copy(late).wait_recv()
 
-        chain(1, s)
-        chain(0, s)
+        chain(False, s)
+        chain(True, s)
         return carry
 
     lax.fori_loop(0, CHUNKS + LAG + (CHAIN - 1) * HOP, slot, 0)

time: 54.2 us -> 53.9 us (level)
  no operation moved by 1% of the time
where the time goes in v5:
time: 53.9 us; the launch traced here: 53.5 us
  Pallas kernels  52.4 us (97%)
  between operations  0.64 us (1%)
    pallas_call x1, Pallas kernels, shards(): pl.pallas_call(functools.partial(kernel, (kd, kt, width)), out_shape=pltp...  52.4 us

profile of v5, /device:TPU:8, one launch (start us, length us, event | category | flops | bytes accessed | tf_op | source)
XLA Modules:
  0.0 53.5 jit_solution(4264494729519932732)
XLA Ops:
  0.6 52.4 %verify.1 = f32[4,16]{1,0:T(4,128)S(1)} custom-call(bf16[4,512]{1,0:T(4,128)(2,1)} %dh.1, bf16[4,1024]{1,0:T(4,128)(2,1)} %th.1, f32[1,512]{1,0:T(1,128)} %bitcast.14, f32[1,1024]{1,0:T(1,128)} %bitcast.13, bf16[4008,512]{1,0:T(8,128)(2,1)} %bitcast.11, bf16[4008,1024]{1,0:T(8,128)(2,1)} %bitcast.10, s32[1,4008]{1,0:T(1,128)} %bitcast.12, s32[128]{0:T(128)} %bits_hbm.1, ...), custom_call_target="tpu_custom_call" | custom-call | tf_op jit(solution)/shard_map/verify/pallas_call | solution.py:515
  53.0 0.5 bitcast_subtract_fusion
